TPU v7x, 32 devices: a whole 2x2x4 slice. The times are simulated.
32 devices in a mesh: face: 2 (over y), fy: 4 (over x, core), fx: 4 (over z).
Axes of the slice: x: 2, y: 2, z: 4, core: 2. Of those that a mesh axis runs over, the one named last changes fastest.
Arguments:
- state: float32 [6, 32, 32, 192], P('face', 'fy', 'fx'), may hold values from -6 to 6
- jacobian: float32 [6, 32, 32], P('face', 'fy', 'fx'), may hold values from 0.5 to 2
- metric_diag: float32 [2, 6, 32, 32], P(None, 'face', 'fy', 'fx'), may hold values from 0.6 to 1.4
- metric_cross: float32 [6, 32, 32], P('face', 'fy', 'fx'), may hold values from -0.3 to 0.3
- coriolis: float32 [6, 32, 32], P('face', 'fy', 'fx'), may hold values from -2 to 2
- nbr_face: int32 [6, 4], replicated, may hold values from 0 to 5, as said below
- nbr_edge: int32 [6, 4], replicated, may hold values from 0 to 3, as said below
Outputs:
- updated: float32 [6, 32, 32, 192], P('face', 'fy', 'fx')
Inputs may be any that keep to these rules, and one draw needn't show every extreme that they name: Edge e of a face is 0 south (row 0), 1 east (last column), 2 north (last row), 3 west (column 0). Edge e of face f is glued to edge nbr_edge[f, e] of face nbr_face[f, e], and that edge back to it; the 6 faces are glued as the surface of a cube, three faces at each corner, the two glued edges running in opposite senses when both are read counterclockwise. `nbr_edge`: see nbr_face.
All inputs are finite; a program needn't handle non-finite values.
Results may differ from a plain program's by a relative error of at most 0.0001.
Values sent between devices are 32-bit elements; how exact they have to be, the bound alone decides.
A program may use at most 64 MiB of HBM per device.

v0:
```python
import jax
import jax.numpy as jnp
import numpy as np
from jax import lax
from jax.sharding import PartitionSpec as P

time_step = 0.05
hyper_coeff = 0.0005


def padded(cells, sides, width):
    for axis, dim in sides:
        count = lax.axis_size(axis)
        ends = count - 1
        head = lax.slice_in_dim(cells, 0, width, axis=dim)
        tail = lax.slice_in_dim(cells, cells.shape[dim] - width, cells.shape[dim], axis=dim)
        cells = jnp.concatenate(
            [
                lax.ppermute(tail, axis, [(i, (i + 1) % count) for i in range(ends)]),
                cells,
                lax.ppermute(head, axis, [((i + 1) % count, i) for i in range(ends)]),
            ],
            axis=dim,
        )
    return cells


def deriv_table():
    gll_nodes = np.array([-1.0, -1.0 / np.sqrt(5.0), 1.0 / np.sqrt(5.0), 1.0])
    bary_weights = np.ones(4)
    for j in range(4):
        for m in range(4):
            if m != j:
                bary_weights[j] = bary_weights[j] / (gll_nodes[j] - gll_nodes[m])
    matrix = np.zeros((4, 4))
    for i in range(4):
        for j in range(4):
            if i != j:
                matrix[i, j] = bary_weights[j] / bary_weights[i] / (gll_nodes[i] - gll_nodes[j])
        matrix[i, i] = -np.sum(matrix[i])
    return matrix


def along_x(values):
    face_count, row_count, col_count, chan_count = values.shape
    blocks = values.reshape(face_count, row_count, col_count // 4, 4, chan_count)
    result = jnp.einsum(
        "jk,abekc->abejc",
        jnp.asarray(deriv_table(), jnp.float32),
        blocks,
        precision=lax.Precision.HIGHEST,
    )
    return result.reshape(values.shape)


def along_y(values):
    face_count, row_count, col_count, chan_count = values.shape
    blocks = values.reshape(face_count, row_count // 4, 4, col_count, chan_count)
    result = jnp.einsum(
        "ik,aekxc->aeixc",
        jnp.asarray(deriv_table(), jnp.float32),
        blocks,
        precision=lax.Precision.HIGHEST,
    )
    return result.reshape(values.shape)


def mass_of(jacobian):
    weights = jnp.asarray([1.0 / 6.0, 5.0 / 6.0, 5.0 / 6.0, 1.0 / 6.0], jnp.float32)
    row_weight = jnp.tile(weights, jacobian.shape[1] // 4)
    col_weight = jnp.tile(weights, jacobian.shape[2] // 4)
    return jacobian * row_weight[None, :, None] * col_weight[None, None, :]


def tendency(state, geometry, planet):
    volume, metric_xx, metric_yy, metric_xy = geometry
    levels = state.shape[-1] // 3
    wind_u = state[..., :levels]
    wind_v = state[..., levels : 2 * levels]
    temper = state[..., 2 * levels :]
    contra_u = metric_xx * wind_u + metric_xy * wind_v
    contra_v = metric_xy * wind_u + metric_yy * wind_v
    energy = 0.5 * (wind_u * contra_u + wind_v * contra_v) + temper
    xderivs = along_x(jnp.concatenate([wind_v, temper, energy], -1))
    yderivs = along_y(jnp.concatenate([wind_u, temper, energy], -1))
    absolute = (xderivs[..., :levels] - yderivs[..., :levels]) / volume + planet
    tend_u = absolute * volume * contra_v - xderivs[..., 2 * levels :]
    tend_v = -absolute * volume * contra_u - yderivs[..., 2 * levels :]
    tend_t = -(
        contra_u * xderivs[..., levels : 2 * levels] + contra_v * yderivs[..., levels : 2 * levels]
    )
    return state + time_step * jnp.concatenate([tend_u, tend_v, tend_t], -1)


def laplace(values, geometry):
    volume, metric_xx, metric_yy, metric_xy = geometry
    grad_x = along_x(values)
    grad_y = along_y(values)
    flux_x = volume * (metric_xx * grad_x + metric_xy * grad_y)
    flux_y = volume * (metric_xy * grad_x + metric_yy * grad_y)
    return (along_x(flux_x) + along_y(flux_y)) / volume


def combine(values, axis):
    length = values.shape[axis] - 2
    positions = jnp.arange(length)
    leading = (positions % 4 == 0).astype(jnp.float32)
    trailing = (positions % 4 == 3).astype(jnp.float32)
    broad_shape = [1, 1, 1, 1]
    broad_shape[axis] = length
    leading = leading.reshape(broad_shape)
    trailing = trailing.reshape(broad_shape)
    middle = lax.slice_in_dim(values, 1, length + 1, axis=axis)
    previous = lax.slice_in_dim(values, 0, length, axis=axis)
    following = lax.slice_in_dim(values, 2, length + 2, axis=axis)
    return middle + leading * previous + trailing * following


def rotate(segment, quarter, levels):
    cosine = ((quarter == 0).astype(jnp.float32) - (quarter == 2).astype(jnp.float32))[..., None]
    sine_part = ((quarter == 1).astype(jnp.float32) - (quarter == 3).astype(jnp.float32))[..., None]
    wind_u = segment[..., :levels]
    wind_v = segment[..., levels : 2 * levels]
    return jnp.concatenate(
        [
            cosine * wind_u - sine_part * wind_v,
            sine_part * wind_u + cosine * wind_v,
            segment[..., 2 * levels :],
        ],
        -1,
    )


def in_face(values):
    across = combine(padded(values, (("fx", 2),), 1), 2)
    return combine(padded(across, (("fy", 1),), 1), 1)


def place_pieces(
    got_flat,
    got_tall,
    vector,
    nbr_edge,
    flat_edge,
    tall_edge,
    on_south,
    on_west,
    flat_start,
    tall_start,
    face_local,
    side_nodes,
    chan_count,
    levels,
):
    edge_ids = jnp.arange(4, dtype=jnp.int32)
    flat_target = nbr_edge[:, flat_edge]
    tall_target = nbr_edge[:, tall_edge]
    if vector:
        got_flat = rotate(got_flat, ((flat_target - flat_edge + 2) % 4)[None, :, None], levels)
        got_tall = rotate(got_tall, ((tall_target - tall_edge + 2) % 4)[None, :, None], levels)
    got_flat = jnp.where(on_south, got_flat[:, :, ::-1], got_flat)
    got_tall = jnp.where(on_west, got_tall, got_tall[:, :, ::-1])
    flat_pick = (flat_target[:, None] == edge_ids[None, :]).astype(jnp.float32)
    tall_pick = (tall_target[:, None] == edge_ids[None, :]).astype(jnp.float32)
    flat_rims = jnp.einsum("se,gsjc->gejc", flat_pick, got_flat, precision=lax.Precision.HIGHEST)
    tall_rims = jnp.einsum("se,gsjc->gejc", tall_pick, got_tall, precision=lax.Precision.HIGHEST)
    empty_rims = jnp.zeros((face_local, 4, side_nodes, chan_count), jnp.float32)
    rim_strips = lax.dynamic_update_slice(empty_rims, flat_rims, (0, 0, flat_start, 0))
    return rim_strips + lax.dynamic_update_slice(empty_rims, tall_rims, (0, 0, tall_start, 0))


def outgoing(
    summed, nbr_face, face_ids, flat_edge, tall_edge, on_south, on_west, flat_live, tall_live
):
    row_count = summed.shape[1]
    col_count = summed.shape[2]
    all_faces = jnp.arange(nbr_face.shape[0], dtype=jnp.int32)
    flat_piece = jnp.where(on_south, summed[:, 0], summed[:, row_count - 1])
    tall_piece = jnp.where(on_west, summed[:, :, 0], summed[:, :, col_count - 1])
    flat_dest = nbr_face[face_ids, flat_edge]
    tall_dest = nbr_face[face_ids, tall_edge]
    flat_send = ((all_faces[:, None] == flat_dest[None, :]) & flat_live).astype(jnp.float32)
    tall_send = ((all_faces[:, None] == tall_dest[None, :]) & tall_live).astype(jnp.float32)
    return (
        flat_send[:, :, None, None] * flat_piece[None],
        tall_send[:, :, None, None] * tall_piece[None],
    )


def assemble(values, vector, nbr_face, nbr_edge):
    summed = in_face(values)
    face_local, row_count, col_count, chan_count = summed.shape
    levels = chan_count // 3
    row_index = lax.axis_index("fy")
    col_index = lax.axis_index("fx")
    side_nodes = row_count * lax.axis_size("fy")
    face_ids = lax.axis_index("face") * face_local + jnp.arange(face_local, dtype=jnp.int32)
    on_south = row_index == 0
    on_north = row_index == lax.axis_size("fy") - 1
    on_west = col_index == 0
    on_east = col_index == lax.axis_size("fx") - 1
    flat_live = on_south | on_north
    tall_live = on_west | on_east
    flat_edge = jnp.where(on_south, 0, 2).astype(jnp.int32)
    tall_edge = jnp.where(on_west, 3, 1).astype(jnp.int32)
    flat_start = jnp.where(
        on_south, side_nodes - (col_index + 1) * col_count, col_index * col_count
    )
    tall_start = jnp.where(on_west, row_index * row_count, side_nodes - (row_index + 1) * row_count)
    send_flat, send_tall = outgoing(
        summed, nbr_face, face_ids, flat_edge, tall_edge, on_south, on_west, flat_live, tall_live
    )
    got_flat, got_tall = (
        lax.all_to_all(send_flat, "face", split_axis=0, concat_axis=1, tiled=True),
        lax.all_to_all(send_tall, "face", split_axis=0, concat_axis=1, tiled=True),
    )
    rim_strips = place_pieces(
        got_flat,
        got_tall,
        vector,
        nbr_edge,
        flat_edge,
        tall_edge,
        on_south,
        on_west,
        flat_start,
        tall_start,
        face_local,
        side_nodes,
        chan_count,
        levels,
    )
    flat_lines = jnp.stack([rim_strips[:, 0], rim_strips[:, 2, ::-1]], axis=1)
    flat_lines = flat_lines.reshape(face_local, 2, lax.axis_size("fx"), col_count, chan_count)
    tall_lines = jnp.stack([rim_strips[:, 1], rim_strips[:, 3, ::-1]], axis=1)
    tall_lines = tall_lines.reshape(face_local, 2, lax.axis_size("fy"), row_count, chan_count)
    flat_whole = lax.psum(flat_lines, "fy")
    tall_whole = lax.psum(tall_lines, "fx")
    flat_block = lax.psum_scatter(flat_whole, "fx", scatter_dimension=2, tiled=True)
    tall_block = lax.psum_scatter(tall_whole, "fy", scatter_dimension=2, tiled=True)
    flat_add = jnp.where(on_south, flat_block[:, 0, 0], flat_block[:, 1, 0])
    tall_add = jnp.where(on_west, tall_block[:, 1, 0], tall_block[:, 0, 0])
    result = summed.at[:, 0].add(jnp.where(on_south, flat_add, 0.0))
    result = result.at[:, row_count - 1].add(jnp.where(on_north, flat_add, 0.0))
    result = result.at[:, :, 0].add(jnp.where(on_west, tall_add, 0.0))
    result = result.at[:, :, col_count - 1].add(jnp.where(on_east, tall_add, 0.0))
    return result


def per_device(state, jacobian, metric_diag, metric_cross, coriolis, nbr_face, nbr_edge):
    node_mass = mass_of(jacobian)[..., None]
    total_mass = assemble(node_mass, False, nbr_face, nbr_edge)
    geometry = (
        jacobian[..., None],
        metric_diag[0][..., None],
        metric_diag[1][..., None],
        metric_cross[..., None],
    )
    raw = tendency(state, geometry, coriolis[..., None])
    sectioned = assemble(node_mass * raw, True, nbr_face, nbr_edge) / total_mass
    first_lap = (
        assemble(node_mass * laplace(sectioned, geometry), True, nbr_face, nbr_edge) / total_mass
    )
    second_lap = (
        assemble(node_mass * laplace(first_lap, geometry), True, nbr_face, nbr_edge) / total_mass
    )
    return sectioned - hyper_coeff * second_lap


def solution(mesh):
    return jax.shard_map(
        per_device,
        mesh=mesh,
        in_specs=(
            P("face", "fy", "fx", None),
            P("face", "fy", "fx"),
            P(None, "face", "fy", "fx"),
            P("face", "fy", "fx"),
            P("face", "fy", "fx"),
            P(),
            P(),
        ),
        out_specs=P("face", "fy", "fx", None),
        check_vma=False,
    )
```

profile of v0, /device:TPU:0, one launch (start us, length us, event | category | flops | bytes accessed | tf_op | source)
XLA Modules:
  0.0 370.9 jit_solution(3466996314126042414)
XLA Ops:
  8.1 1.0 slice.770
  13.0 1.3 collective-permute-start.1
  14.4 5.6 %collective-permute-start = (f32[3,8,1,192]{3,2,0,1:T(1,128)S(1)}, f32[3,8,1,192]{3,2,0,1:T(1,128)S(1)}, u32[]{:S(2)}, u32[]{:S(2)}) collective-permute-start(f32[3,8,1,192]{3,2,0,1:T(1,128)S(1)} %slice.902), channel_id=1, source_target_pairs={{0,1},{1,2},{2,3},{4,5},{5,6},{6,7},{8,9},{9,10},{10,11},{12,13},{... | collective-permute-start | bytes 55304 | tf_op jit(solution)/shard_map/ppermute | solution.py:19
  20.1 1.3 collective-permute-start.5
  21.4 4.5 %collective-permute-start.4 = (f32[3,8,1,1]{2,1,0,3:T(8,128)S(1)}, f32[3,8,1,1]{2,1,0,3:T(8,128)S(1)}, u32[]{:S(2)}, u32[]{:S(2)}) collective-permute-start(f32[3,8,1,1]{2,1,0,3:T(8,128)S(1)} %get-tuple-element.262), channel_id=1, source_target_pairs={{0,1},{1,2},{2,3},{4,5},{5,6},{6,7},{8,9},{9,10},{10,11},{12,13},{... | collective-permute-start | bytes 296 | tf_op jit(solution)/shard_map/ppermute | solution.py:19
  31.1 1.3 collective-permute-start.7
  32.4 3.0 collective-permute-start.6
  37.2 3.2 all-to-all-start.2
  41.1 3.1 all-to-all-done.2
  44.3 3.2 all-to-all-start.3
  47.6 3.7 all-to-all-done.3
  52.8 1.3 collective-permute-start.3
  54.1 3.0 collective-permute-start.2
  57.2 13.3 %all-reduce.4 = f32[3,2,4,8,1]{3,1,4,0,2:T(2,128)S(1)} all-reduce(f32[3,2,4,8,1]{3,1,4,0,2:T(2,128)S(1)} %copy.284), channel_id=5, replica_groups=mesh['face'=2,'fy'=4,'fx'=4] {'fy'}, use_global_device_ids=true, to_apply=%region_7.8.clone | all-reduce | flops 192 | bytes 1536
  71.4 3.4 all-to-all-start
  75.7 3.7 %all-to-all-done = f32[6,3,8,192]{3,2,1,0:T(8,128)S(1)} async-done(((f32[6,3,8,192]{3,2,1,0:T(8,128)}), f32[6,3,8,192]{3,2,1,0:T(8,128)S(1)}, u32[]{:S(2)}, u32[]{:S(2)}) %all-to-all-start) | async-done | bytes 110624 | tf_op jit(solution)/shard_map/all_to_all | solution.py:214
  79.4 3.4 all-to-all-start.1
  83.3 4.1 %all-to-all-done.1 = f32[6,3,8,192]{3,2,1,0:T(8,128)S(1)} async-done(((f32[6,3,8,192]{3,2,1,0:T(8,128)}), f32[6,3,8,192]{3,2,1,0:T(8,128)S(1)}, u32[]{:S(2)}, u32[]{:S(2)}) %all-to-all-start.1) | async-done | bytes 110624 | tf_op jit(solution)/shard_map/all_to_all | solution.py:215
  91.5 33.0 %all-reduce.13.cloned.1.call-done = f32[3,2,4,8,192]{4,3,0,2,1:T(8,128)} async-done(((f32[3,2,4,8,192]{4,3,0,2,1:T(8,128)}), f32[3,2,4,8,192]{4,3,0,2,1:T(8,128)}) %all-reduce.13.cloned.1.call-update) | async-done | bytes 147472
  124.5 1.4 constant_dynamic-slice_fusion.6
  126.8 18.5 %all-reduce.7 = (f32[3,2,1,8,192]{4,1,3,2,0:T(2,128)S(1)}, f32[3,2,4,8,1]{3,1,4,0,2:T(2,128)S(1)}, f32[3,2,1,8,1]{3,1,4,0,2:T(2,128)S(1)}) all-reduce(f32[3,2,1,8,192]{4,1,3,2,0:T(2,128)S(1)} %copy.277, f32[3,2,4,8,1]{3,1,4,0,2:T(2,128)S(1)} %copy.281, ...), channel_id=1, replica_groups=mesh['face'=2,'fy'=4,'fx'=4] {'fx'}, use_global_device_ids=true, to_apply=%region_2.3 | all-reduce | flops 9456 | bytes 75648 | tf_op jit(solution)/shard_map/psum | solution.py:238
  145.9 10.7 %all-reduce.8 = (f32[3,2,1,8,192]{4,3,0,2,1:T(8,128)S(1)}, f32[3,2,1,8,1]{3,1,4,0,2:T(2,128)S(1)}) all-reduce(f32[3,2,1,8,192]{4,3,0,2,1:T(8,128)S(1)} %constant_dynamic-slice_fusion.6, f32[3,2,1,8,1]{3,1,4,0,2:T(2,128)S(1)} %constant_dynamic-slice_fusion.5), channel_id=1, replica_groups=mesh['face'=2,'fy'=4,'fx'=4] {'fy'}, use_global_device_ids=true, to_apply=%region_0.1 | all-reduce | flops 9264 | bytes 74112 | tf_op jit(solution)/shard_map/psum | solution.py:237
  160.6 1.3 collective-permute-start.9
  161.9 4.5 %collective-permute-start.8 = (f32[3,8,1,192]{3,2,0,1:T(1,128)S(1)}, f32[3,8,1,192]{3,2,0,1:T(1,128)S(1)}, u32[]{:S(2)}, u32[]{:S(2)}) collective-permute-start(f32[3,8,1,192]{3,2,0,1:T(1,128)S(1)} %get-tuple-element.230), channel_id=1, source_target_pairs={{0,1},{1,2},{2,3},{4,5},{5,6},{6,7},{8,9},{9,10},{10,11},{12,13},{... | collective-permute-start | bytes 55304 | tf_op jit(solution)/shard_map/ppermute | solution.py:19
  166.4 1.5 collective-permute-done.8
  168.0 1.3 collective-permute-start.11
  169.3 3.2 collective-permute-start.10
  174.1 3.4 all-to-all-start.4
  178.3 4.0 %all-to-all-done.4 = f32[6,3,8,192]{3,2,1,0:T(8,128)S(1)} async-done(((f32[6,3,8,192]{3,2,1,0:T(8,128)}), f32[6,3,8,192]{3,2,1,0:T(8,128)S(1)}, u32[]{:S(2)}, u32[]{:S(2)}) %all-to-all-start.4) | async-done | bytes 110624 | tf_op jit(solution)/shard_map/all_to_all | solution.py:214
  182.3 3.4 all-to-all-start.5
  186.2 4.3 %all-to-all-done.5 = f32[6,3,8,192]{3,2,1,0:T(8,128)S(1)} async-done(((f32[6,3,8,192]{3,2,1,0:T(8,128)}), f32[6,3,8,192]{3,2,1,0:T(8,128)S(1)}, u32[]{:S(2)}, u32[]{:S(2)}) %all-to-all-start.5) | async-done | bytes 110624 | tf_op jit(solution)/shard_map/all_to_all | solution.py:215
  193.8 35.0 %all-reduce.15.cloned.1.call-done = f32[3,2,4,8,192]{4,3,0,2,1:T(8,128)} async-done(((f32[3,2,4,8,192]{4,3,0,2,1:T(8,128)}), f32[3,2,4,8,192]{4,3,0,2,1:T(8,128)}) %all-reduce.15.cloned.1.call-update) | async-done | bytes 147472
  228.8 1.4 constant_dynamic-slice_fusion.3
  230.3 10.5 %psum.68 = f32[3,2,1,8,192]{4,3,0,2,1:T(8,128)S(1)} all-reduce(f32[3,2,1,8,192]{4,3,0,2,1:T(8,128)S(1)} %constant_dynamic-slice_fusion.3), channel_id=1, replica_groups=mesh['face'=2,'fy'=4,'fx'=4] {'fy'}, use_global_device_ids=true, to_apply=%region_8.9 | all-reduce | flops 9216 | bytes 73728 | tf_op jit(solution)/shard_map/psum | solution.py:237
  241.7 18.2 %psum.69 = f32[3,2,1,8,192]{4,1,3,2,0:T(2,128)S(1)} all-reduce(f32[3,2,1,8,192]{4,1,3,2,0:T(2,128)S(1)} %copy.314), channel_id=1, replica_groups=mesh['face'=2,'fy'=4,'fx'=4] {'fx'}, use_global_device_ids=true, to_apply=%region_10.11 | all-reduce | flops 9216 | bytes 73728 | tf_op jit(solution)/shard_map/psum | solution.py:238
  263.2 1.3 collective-permute-start.13
  264.5 4.5 %collective-permute-start.12 = (f32[3,8,1,192]{3,2,0,1:T(1,128)S(1)}, f32[3,8,1,192]{3,2,0,1:T(1,128)S(1)}, u32[]{:S(2)}, u32[]{:S(2)}) collective-permute-start(f32[3,8,1,192]{3,2,0,1:T(1,128)S(1)} %get-tuple-element.226), channel_id=1, source_target_pairs={{0,1},{1,2},{2,3},{4,5},{5,6},{6,7},{8,9},{9,10},{10,11},{12,13},{... | collective-permute-start | bytes 55304 | tf_op jit(solution)/shard_map/ppermute | solution.py:19
  269.0 1.5 collective-permute-done.12
  270.6 1.3 collective-permute-start.15
  271.9 3.0 collective-permute-start.14
  276.7 3.4 all-to-all-start.6
  280.9 4.0 %all-to-all-done.6 = f32[6,3,8,192]{3,2,1,0:T(8,128)S(1)} async-done(((f32[6,3,8,192]{3,2,1,0:T(8,128)}), f32[6,3,8,192]{3,2,1,0:T(8,128)S(1)}, u32[]{:S(2)}, u32[]{:S(2)}) %all-to-all-start.6) | async-done | bytes 110624 | tf_op jit(solution)/shard_map/all_to_all | solution.py:214
  284.9 3.4 all-to-all-start.7
  288.9 4.2 %all-to-all-done.7 = f32[6,3,8,192]{3,2,1,0:T(8,128)S(1)} async-done(((f32[6,3,8,192]{3,2,1,0:T(8,128)}), f32[6,3,8,192]{3,2,1,0:T(8,128)S(1)}, u32[]{:S(2)}, u32[]{:S(2)}) %all-to-all-start.7) | async-done | bytes 110624 | tf_op jit(solution)/shard_map/all_to_all | solution.py:215
  296.4 34.9 %all-reduce.17.cloned.1.call-done = f32[3,2,4,8,192]{4,3,0,2,1:T(8,128)} async-done(((f32[3,2,4,8,192]{4,3,0,2,1:T(8,128)}), f32[3,2,4,8,192]{4,3,0,2,1:T(8,128)}) %all-reduce.17.cloned.1.call-update) | async-done | bytes 147472
  331.3 1.4 constant_dynamic-slice_fusion.2
  332.8 10.5 %psum.70 = f32[3,2,1,8,192]{4,3,0,2,1:T(8,128)S(1)} all-reduce(f32[3,2,1,8,192]{4,3,0,2,1:T(8,128)S(1)} %constant_dynamic-slice_fusion.2), channel_id=1, replica_groups=mesh['face'=2,'fy'=4,'fx'=4] {'fy'}, use_global_device_ids=true, to_apply=%region_12.13 | all-reduce | flops 9216 | bytes 73728 | tf_op jit(solution)/shard_map/psum | solution.py:237
  344.2 18.2 %psum.71 = f32[3,2,1,8,192]{4,1,3,2,0:T(2,128)S(1)} all-reduce(f32[3,2,1,8,192]{4,1,3,2,0:T(2,128)S(1)} %copy.330), channel_id=1, replica_groups=mesh['face'=2,'fy'=4,'fx'=4] {'fx'}, use_global_device_ids=true, to_apply=%region_14.15 | all-reduce | flops 9216 | bytes 73728 | tf_op jit(solution)/shard_map/psum | solution.py:238
  (268 shorter events, 43.5 us)
Async XLA Ops:
  7.4 19.6 %copy-start = (s32[6,4]{0,1:T(4,128)S(1)}, s32[6,4]{0,1:T(4,128)}, u32[]{:S(2)}) copy-start(s32[6,4]{0,1:T(4,128)} %param.55) | copy-start | bytes 292
  7.4 1.8 copy-start.1
  8.1 1.0 copy-start.3
  9.5 0.7 copy-start.4
  11.2 0.7 copy-start.9
  11.2 0.7 copy-start.2
  12.0 0.7 copy-start.5
  13.0 39.6 %collective-permute-start.1 = (f32[3,8,1,192]{3,2,1,0:T(1,128)S(1)}, f32[3,8,1,192]{3,2,1,0:T(1,128)S(1)}, u32[]{:S(2)}, u32[]{:S(2)}) collective-permute-start(f32[3,8,1,192]{3,2,1,0:T(1,128)S(1)} %slice.903), channel_id=1, source_target_pairs={{1,0},{2,1},{3,2},{5,4},{6,5},{7,6},{9,8},{10,9},{11,10},{13,12},{... | collective-permute-start | bytes 55304 | tf_op jit(solution)/shard_map/ppermute | solution.py:21
  14.4 38.2 %collective-permute-start = (f32[3,8,1,192]{3,2,0,1:T(1,128)S(1)}, f32[3,8,1,192]{3,2,0,1:T(1,128)S(1)}, u32[]{:S(2)}, u32[]{:S(2)}) collective-permute-start(f32[3,8,1,192]{3,2,0,1:T(1,128)S(1)} %slice.902), channel_id=1, source_target_pairs={{0,1},{1,2},{2,3},{4,5},{5,6},{6,7},{8,9},{9,10},{10,11},{12,13},{... | collective-permute-start | bytes 55304 | tf_op jit(solution)/shard_map/ppermute | solution.py:19
  20.1 10.9 %collective-permute-start.5 = (f32[3,8,1,1]{2,1,0,3:T(8,128)S(1)}, f32[3,8,1,1]{2,1,0,3:T(8,128)S(1)}, u32[]{:S(2)}, u32[]{:S(2)}) collective-permute-start(f32[3,8,1,1]{2,1,0,3:T(8,128)S(1)} %get-tuple-element.263), channel_id=1, source_target_pairs={{1,0},{2,1},{3,2},{5,4},{6,5},{7,6},{9,8},{10,9},{11,10},{13,12},{... | collective-permute-start | bytes 296 | tf_op jit(solution)/shard_map/ppermute | solution.py:21
  21.4 9.6 %collective-permute-start.4 = (f32[3,8,1,1]{2,1,0,3:T(8,128)S(1)}, f32[3,8,1,1]{2,1,0,3:T(8,128)S(1)}, u32[]{:S(2)}, u32[]{:S(2)}) collective-permute-start(f32[3,8,1,1]{2,1,0,3:T(8,128)S(1)} %get-tuple-element.262), channel_id=1, source_target_pairs={{0,1},{1,2},{2,3},{4,5},{5,6},{6,7},{8,9},{9,10},{10,11},{12,13},{... | collective-permute-start | bytes 296 | tf_op jit(solution)/shard_map/ppermute | solution.py:19
  26.0 0.7 copy-start.6
  28.3 0.7 copy-start.8
  28.9 0.7 copy-start.7
  31.1 4.3 %collective-permute-start.7 = (f32[3,1,8,1]{2,1,0,3:T(1,128)S(1)}, f32[3,1,8,1]{2,1,0,3:T(1,128)S(1)}, u32[]{:S(2)}, u32[]{:S(2)}) collective-permute-start(f32[3,1,8,1]{2,1,0,3:T(1,128)S(1)} %get-tuple-element.261), channel_id=1, source_target_pairs={{4,0},{8,4},{12,8},{5,1},{9,5},{13,9},{6,2},{10,6},{14,10},{7,3},{... | collective-permute-start | bytes 296 | tf_op jit(solution)/shard_map/ppermute | solution.py:21
  32.4 3.8 %collective-permute-start.6 = (f32[3,1,8,1]{2,1,0,3:T(1,128)S(1)}, f32[3,1,8,1]{2,1,0,3:T(1,128)S(1)}, u32[]{:S(2)}, u32[]{:S(2)}) collective-permute-start(f32[3,1,8,1]{2,1,0,3:T(1,128)S(1)} %get-tuple-element.260), channel_id=1, source_target_pairs={{0,4},{4,8},{8,12},{1,5},{5,9},{9,13},{2,6},{6,10},{10,14},{3,7},{... | collective-permute-start | bytes 296 | tf_op jit(solution)/shard_map/ppermute | solution.py:19
  37.2 7.0 %all-to-all-start.2 = ((f32[6,3,8,1]{2,3,1,0:T(1,128)}), f32[6,3,8,1]{2,3,1,0:T(1,128)S(1)}, u32[]{:S(2)}, u32[]{:S(2)}) async-start(f32[6,3,8,1]{2,3,1,0:T(1,128)} %broadcast_multiply_fusion.7), calls=%async_computation.2 | async-start | bytes 18432 | tf_op jit(solution)/shard_map/all_to_all | solution.py:214
  44.3 7.0 %all-to-all-start.3 = ((f32[6,3,8,1]{2,3,1,0:T(1,128)}), f32[6,3,8,1]{2,3,1,0:T(1,128)S(1)}, u32[]{:S(2)}, u32[]{:S(2)}) async-start(f32[6,3,8,1]{2,3,1,0:T(1,128)} %broadcast_multiply_fusion.6), calls=%async_computation.3 | async-start | bytes 18432 | tf_op jit(solution)/shard_map/all_to_all | solution.py:215
  52.8 17.7 %collective-permute-start.3 = (f32[3,1,8,192]{3,2,1,0:T(8,128)S(1)}, f32[3,1,8,192]{3,2,1,0:T(8,128)S(1)}, u32[]{:S(2)}, u32[]{:S(2)}) collective-permute-start(f32[3,1,8,192]{3,2,1,0:T(8,128)S(1)} %slice.905), channel_id=1, source_target_pairs={{4,0},{8,4},{12,8},{5,1},{9,5},{13,9},{6,2},{10,6},{14,10},{7,3},{... | collective-permute-start | bytes 55304 | tf_op jit(solution)/shard_map/ppermute | solution.py:21
  54.1 16.4 %collective-permute-start.2 = (f32[3,1,8,192]{3,2,0,1:T(8,128)S(1)}, f32[3,1,8,192]{3,2,0,1:T(8,128)S(1)}, u32[]{:S(2)}, u32[]{:S(2)}) collective-permute-start(f32[3,1,8,192]{3,2,0,1:T(8,128)S(1)} %slice.904), channel_id=1, source_target_pairs={{0,4},{4,8},{8,12},{1,5},{5,9},{9,13},{2,6},{6,10},{10,14},{3,7},{... | collective-permute-start | bytes 55304 | tf_op jit(solution)/shard_map/ppermute | solution.py:19
  71.4 8.0 %all-to-all-start = ((f32[6,3,8,192]{3,2,1,0:T(8,128)}), f32[6,3,8,192]{3,2,1,0:T(8,128)S(1)}, u32[]{:S(2)}, u32[]{:S(2)}) async-start(f32[6,3,8,192]{3,2,1,0:T(8,128)} %broadcast_multiply_fusion.5), calls=%async_computation | async-start | bytes 294912 | tf_op jit(solution)/shard_map/all_to_all | solution.py:214
  79.4 8.0 %all-to-all-start.1 = ((f32[6,3,8,192]{3,2,1,0:T(8,128)}), f32[6,3,8,192]{3,2,1,0:T(8,128)S(1)}, u32[]{:S(2)}, u32[]{:S(2)}) async-start(f32[6,3,8,192]{3,2,1,0:T(8,128)} %broadcast_multiply_fusion.4), calls=%async_computation.1 | async-start | bytes 294912 | tf_op jit(solution)/shard_map/all_to_all | solution.py:215
  82.8 41.7 %all-reduce.13.cloned.1.call-start = ((), (), s32[]{:S(2)}) async-start(), calls=%async_computation.14 | async-start | bytes 393216
  89.7 36.3 %reduce-scatter.7.cloned.1.call-start = ((), (), s32[]{:S(2)}) async-start(), calls=%async_computation.11 | async-start | bytes 245760 | tf_op jit(solution)/shard_map/reduce_scatter | solution.py:240
  160.6 5.9 %collective-permute-start.9 = (f32[3,8,1,192]{3,2,0,1:T(1,128)S(1)}, f32[3,8,1,192]{3,2,0,1:T(1,128)S(1)}, u32[]{:S(2)}, u32[]{:S(2)}) collective-permute-start(f32[3,8,1,192]{3,2,0,1:T(1,128)S(1)} %get-tuple-element.231), channel_id=1, source_target_pairs={{1,0},{2,1},{3,2},{5,4},{6,5},{7,6},{9,8},{10,9},{11,10},{13,12},{... | collective-permute-start | bytes 55304 | tf_op jit(solution)/shard_map/ppermute | solution.py:21
  161.9 6.1 %collective-permute-start.8 = (f32[3,8,1,192]{3,2,0,1:T(1,128)S(1)}, f32[3,8,1,192]{3,2,0,1:T(1,128)S(1)}, u32[]{:S(2)}, u32[]{:S(2)}) collective-permute-start(f32[3,8,1,192]{3,2,0,1:T(1,128)S(1)} %get-tuple-element.230), channel_id=1, source_target_pairs={{0,1},{1,2},{2,3},{4,5},{5,6},{6,7},{8,9},{9,10},{10,11},{12,13},{... | collective-permute-start | bytes 55304 | tf_op jit(solution)/shard_map/ppermute | solution.py:19
  168.0 4.5 %collective-permute-start.11 = (f32[3,1,8,192]{3,2,0,1:T(8,128)S(1)}, f32[3,1,8,192]{3,2,0,1:T(8,128)S(1)}, u32[]{:S(2)}, u32[]{:S(2)}) collective-permute-start(f32[3,1,8,192]{3,2,0,1:T(8,128)S(1)} %get-tuple-element.229), channel_id=1, source_target_pairs={{4,0},{8,4},{12,8},{5,1},{9,5},{13,9},{6,2},{10,6},{14,10},{7,3},{... | collective-permute-start | bytes 55304 | tf_op jit(solution)/shard_map/ppermute | solution.py:21
  169.3 3.9 %collective-permute-start.10 = (f32[3,1,8,192]{3,2,0,1:T(8,128)S(1)}, f32[3,1,8,192]{3,2,0,1:T(8,128)S(1)}, u32[]{:S(2)}, u32[]{:S(2)}) collective-permute-start(f32[3,1,8,192]{3,2,0,1:T(8,128)S(1)} %get-tuple-element.228), channel_id=1, source_target_pairs={{0,4},{4,8},{8,12},{1,5},{5,9},{9,13},{2,6},{6,10},{10,14},{3,7},{... | collective-permute-start | bytes 55304 | tf_op jit(solution)/shard_map/ppermute | solution.py:19
  174.1 8.2 %all-to-all-start.4 = ((f32[6,3,8,192]{3,2,1,0:T(8,128)}), f32[6,3,8,192]{3,2,1,0:T(8,128)S(1)}, u32[]{:S(2)}, u32[]{:S(2)}) async-start(f32[6,3,8,192]{3,2,1,0:T(8,128)} %broadcast_multiply_fusion.3), calls=%async_computation.4 | async-start | bytes 294912 | tf_op jit(solution)/shard_map/all_to_all | solution.py:214
  182.3 8.2 %all-to-all-start.5 = ((f32[6,3,8,192]{3,2,1,0:T(8,128)}), f32[6,3,8,192]{3,2,1,0:T(8,128)S(1)}, u32[]{:S(2)}, u32[]{:S(2)}) async-start(f32[6,3,8,192]{3,2,1,0:T(8,128)} %broadcast_multiply_fusion.2), calls=%async_computation.5 | async-start | bytes 294912 | tf_op jit(solution)/shard_map/all_to_all | solution.py:215
  185.7 43.1 %all-reduce.15.cloned.1.call-start = ((), (), s32[]{:S(2)}) async-start(), calls=%async_computation.15 | async-start | bytes 393216
  192.8 48.1 %reduce-scatter.9.cloned.1.call-start = ((), (), s32[]{:S(2)}) async-start(), calls=%async_computation.12 | async-start | bytes 245760 | tf_op jit(solution)/shard_map/reduce_scatter | solution.py:240
  263.2 5.9 %collective-permute-start.13 = (f32[3,8,1,192]{3,2,0,1:T(1,128)S(1)}, f32[3,8,1,192]{3,2,0,1:T(1,128)S(1)}, u32[]{:S(2)}, u32[]{:S(2)}) collective-permute-start(f32[3,8,1,192]{3,2,0,1:T(1,128)S(1)} %get-tuple-element.227), channel_id=1, source_target_pairs={{1,0},{2,1},{3,2},{5,4},{6,5},{7,6},{9,8},{10,9},{11,10},{13,12},{... | collective-permute-start | bytes 55304 | tf_op jit(solution)/shard_map/ppermute | solution.py:21
  264.5 6.1 %collective-permute-start.12 = (f32[3,8,1,192]{3,2,0,1:T(1,128)S(1)}, f32[3,8,1,192]{3,2,0,1:T(1,128)S(1)}, u32[]{:S(2)}, u32[]{:S(2)}) collective-permute-start(f32[3,8,1,192]{3,2,0,1:T(1,128)S(1)} %get-tuple-element.226), channel_id=1, source_target_pairs={{0,1},{1,2},{2,3},{4,5},{5,6},{6,7},{8,9},{9,10},{10,11},{12,13},{... | collective-permute-start | bytes 55304 | tf_op jit(solution)/shard_map/ppermute | solution.py:19
  270.6 4.3 %collective-permute-start.15 = (f32[3,1,8,192]{3,2,0,1:T(8,128)S(1)}, f32[3,1,8,192]{3,2,0,1:T(8,128)S(1)}, u32[]{:S(2)}, u32[]{:S(2)}) collective-permute-start(f32[3,1,8,192]{3,2,0,1:T(8,128)S(1)} %get-tuple-element.225), channel_id=1, source_target_pairs={{4,0},{8,4},{12,8},{5,1},{9,5},{13,9},{6,2},{10,6},{14,10},{7,3},{... | collective-permute-start | bytes 55304 | tf_op jit(solution)/shard_map/ppermute | solution.py:21
  271.9 3.9 %collective-permute-start.14 = (f32[3,1,8,192]{3,2,0,1:T(8,128)S(1)}, f32[3,1,8,192]{3,2,0,1:T(8,128)S(1)}, u32[]{:S(2)}, u32[]{:S(2)}) collective-permute-start(f32[3,1,8,192]{3,2,0,1:T(8,128)S(1)} %get-tuple-element.224), channel_id=1, source_target_pairs={{0,4},{4,8},{8,12},{1,5},{5,9},{9,13},{2,6},{6,10},{10,14},{3,7},{... | collective-permute-start | bytes 55304 | tf_op jit(solution)/shard_map/ppermute | solution.py:19
  276.7 8.2 %all-to-all-start.6 = ((f32[6,3,8,192]{3,2,1,0:T(8,128)}), f32[6,3,8,192]{3,2,1,0:T(8,128)S(1)}, u32[]{:S(2)}, u32[]{:S(2)}) async-start(f32[6,3,8,192]{3,2,1,0:T(8,128)} %broadcast_multiply_fusion.1), calls=%async_computation.6 | async-start | bytes 294912 | tf_op jit(solution)/shard_map/all_to_all | solution.py:214
  284.9 8.2 %all-to-all-start.7 = ((f32[6,3,8,192]{3,2,1,0:T(8,128)}), f32[6,3,8,192]{3,2,1,0:T(8,128)S(1)}, u32[]{:S(2)}, u32[]{:S(2)}) async-start(f32[6,3,8,192]{3,2,1,0:T(8,128)} %broadcast_multiply_fusion), calls=%async_computation.7 | async-start | bytes 294912 | tf_op jit(solution)/shard_map/all_to_all | solution.py:215
  288.4 43.0 %all-reduce.17.cloned.1.call-start = ((), (), s32[]{:S(2)}) async-start(), calls=%async_computation.16 | async-start | bytes 393216
  295.4 48.0 %reduce-scatter.11.cloned.1.call-start = ((), (), s32[]{:S(2)}) async-start(), calls=%async_computation.13 | async-start | bytes 245760 | tf_op jit(solution)/shard_map/reduce_scatter | solution.py:240
Sparse Core Ops, SparseCore 0:
  89.8 34.6 all-reduce.12
  192.9 35.8 all-reduce.14
  295.5 35.7 all-reduce.16
Sparse Core Ops, SparseCore 1:
  92.6 19.4 reduce-scatter.6
  195.7 20.6 reduce-scatter.8
  298.3 20.6 reduce-scatter.10
where the time goes:
time: 373 us; the launch traced here: 371 us
  waiting for transfers between devices  139 us (37%)
  blocking collectives  99.7 us (27%)
  starting transfers between devices  69.1 us (19%)
  local copies, waits for them, and re-layouts  26.4 us (7%)
  between operations  16.4 us (4%)
  other arithmetic  12.6 us (3%)
  matrix products  7.16 us (2%)
    unnamed x9, waiting for transfers between devices  103 us
    psum x3, blocking collectives, assemble(): tall_whole = lax.psum(tall_lines, 'fx')  54.8 us
    psum x3, blocking collectives, assemble(): flat_whole = lax.psum(flat_lines, 'fy')  31.7 us
    ppermute x8, starting transfers between devices, padded(): lax.ppermute(tail, axis, [(i, (i + 1) % count) for i in range(ends)])  31.5 us
    all_to_all x4, waiting for transfers between devices, assemble(): lax.all_to_all(send_tall, 'face', split_axis=0, concat_axis=1, tiled=True)  16.2 us
    all_to_all x4, waiting for transfers between devices, assemble(): lax.all_to_all(send_flat, 'face', split_axis=0, concat_axis=1, tiled=True)  14.9 us
    all_to_all x4, starting transfers between devices, assemble(): lax.all_to_all(send_flat, 'face', split_axis=0, concat_axis=1, tiled=True)  13.5 us
    all_to_all x4, starting transfers between devices, assemble(): lax.all_to_all(send_tall, 'face', split_axis=0, concat_axis=1, tiled=True)  13.5 us
  transfers between devices with their start and end apart: 30, of which 16 were waited for; matrix products, arithmetic and copies ran while one was open for 5% of the time, Pallas kernels for 0%

commit v1 on v0

--- a/solution.py
+++ b/solution.py
@@ -235,7 +235,11 @@
     tall_lines = jnp.stack([rim_strips[:, 1], rim_strips[:, 3, ::-1]], axis=1)
     tall_lines = tall_lines.reshape(face_local, 2, lax.axis_size("fy"), row_count, chan_count)
     flat_whole = lax.psum(flat_lines, "fy")
-    tall_whole = lax.psum(tall_lines, "fx")
+    tall_whole = tall_lines
+    for hop in (1, 2):
+        tall_whole = tall_whole + lax.ppermute(
+            tall_whole, "fx", [(dev, dev ^ hop) for dev in range(4)]
+        )
     flat_block = lax.psum_scatter(flat_whole, "fx", scatter_dimension=2, tiled=True)
     tall_block = lax.psum_scatter(tall_whole, "fy", scatter_dimension=2, tiled=True)
     flat_add = jnp.where(on_south, flat_block[:, 0, 0], flat_block[:, 1, 0])

time: 373 us -> 402 us (1.078)
  waiting for transfers between devices: 139 us -> 202 us
  blocking collectives: 99.7 us -> 49.5 us
  starting transfers between devices: 69.1 us -> 86 us
    reduce_scatter x3, waiting for transfers between devices: 0.05 us -> 59 us  [assemble(): lax.psum_scatter(tall_whole, 'fy', scatter_dimension=2, tiled=True)]
    psum x3 -> x0, blocking collectives: 54.8 us -> none  [assemble(): tall_whole = lax.psum(tall_lines, 'fx')]
    ppermute x0 -> x8, starting transfers between devices: none -> 16.9 us  [assemble(): lax.ppermute(tall_whole, 'fx', [(dev, dev ^ hop) for dev in range(4)])]
    ppermute x0 -> x8, waiting for transfers between devices: none -> 11.4 us  [assemble(): lax.ppermute(tall_whole, 'fx', [(dev, dev ^ hop) for dev in range(4)])]
    unnamed x9, waiting for transfers between devices: 103 us -> 95.2 us
    unnamed x1, blocking collectives: 13.3 us -> 17.8 us
    unnamed x33 -> x32, local copies, waits for them, and re-layouts: 10.3 us -> 9.88 us
  transfers between devices with their start and end apart: 30 -> 38, of which waited for: 16 -> 23; matrix products, arithmetic and copies ran while one was open for 5% -> 5% of each run, Pallas kernels for 0% -> 0%
where the time goes in v1:
time: 402 us; the launch traced here: 400 us
  waiting for transfers between devices  202 us (50%)
  starting transfers between devices  86 us (21%)
  blocking collectives  49.5 us (12%)
  local copies, waits for them, and re-layouts  23.8 us (6%)
  between operations  16.4 us (4%)
  other arithmetic  15.5 us (4%)
  matrix products  7.15 us (2%)
    unnamed x9, waiting for transfers between devices  95.2 us
    reduce_scatter x3, waiting for transfers between devices, assemble(): lax.psum_scatter(tall_whole, 'fy', scatter_dimension=2, tiled=True)  59 us
    psum x3, blocking collectives, assemble(): flat_whole = lax.psum(flat_lines, 'fy')  31.7 us
    ppermute x8, starting transfers between devices, padded(): lax.ppermute(tail, axis, [(i, (i + 1) % count) for i in range(ends)])  31.5 us
    unnamed x1, blocking collectives  17.8 us
    ppermute x8, starting transfers between devices, assemble(): lax.ppermute(tall_whole, 'fx', [(dev, dev ^ hop) for dev in range(4)])  16.9 us
    all_to_all x4, waiting for transfers between devices, assemble(): lax.all_to_all(send_tall, 'face', split_axis=0, concat_axis=1, tiled=True)  15.8 us
    all_to_all x4, waiting for transfers between devices, assemble(): lax.all_to_all(send_flat, 'face', split_axis=0, concat_axis=1, tiled=True)  14.8 us
  transfers between devices with their start and end apart: 38, of which 23 were waited for; matrix products, arithmetic and copies ran while one was open for 5% of the time, Pallas kernels for 0%

profile of v1, /device:TPU:0, one launch (start us, length us, event | category | flops | bytes accessed | tf_op | source)
XLA Modules:
  0.0 399.9 jit_solution(4618866222065723823)
XLA Ops:
  14.4 5.6 %collective-permute-start = (f32[3,8,1,192]{3,2,0,1:T(1,128)S(1)}, f32[3,8,1,192]{3,2,0,1:T(1,128)S(1)}, u32[]{:S(2)}, u32[]{:S(2)}) collective-permute-start(f32[3,8,1,192]{3,2,0,1:T(1,128)S(1)} %slice.902), channel_id=1, source_target_pairs={{0,1},{1,2},{2,3},{4,5},{5,6},{6,7},{8,9},{9,10},{10,11},{12,13},{... | collective-permute-start | bytes 55304 | tf_op jit(solution)/shard_map/ppermute | solution.py:19
  21.4 4.5 %collective-permute-start.6 = (f32[3,8,1,1]{2,1,0,3:T(8,128)S(1)}, f32[3,8,1,1]{2,1,0,3:T(8,128)S(1)}, u32[]{:S(2)}, u32[]{:S(2)}) collective-permute-start(f32[3,8,1,1]{2,1,0,3:T(8,128)S(1)} %get-tuple-element.268), channel_id=1, source_target_pairs={{0,1},{1,2},{2,3},{4,5},{5,6},{6,7},{8,9},{9,10},{10,11},{12,13},{... | collective-permute-start | bytes 296 | tf_op jit(solution)/shard_map/ppermute | solution.py:19
  32.4 3.0 collective-permute-start.8
  37.2 3.2 all-to-all-start.2
  41.1 3.1 all-to-all-done.2
  44.2 3.2 all-to-all-start.3
  47.6 3.7 all-to-all-done.3
  52.8 2.5 collective-permute-start.10
  55.3 17.8 %all-reduce.3 = f32[3,2,4,8,1]{3,1,4,0,2:T(2,128)S(1)} all-reduce(f32[3,2,4,8,1]{3,1,4,0,2:T(2,128)S(1)} %copy.287), channel_id=4, replica_groups=mesh['face'=2,'fy'=4,'fx'=4] {'fx'}, use_global_device_ids=true, to_apply=%region_4.5.clone | all-reduce | flops 192 | bytes 1536
  74.7 3.0 collective-permute-start.2
  79.4 3.4 all-to-all-start
  83.7 3.8 all-to-all-done
  87.4 3.4 all-to-all-start.1
  91.3 4.1 %all-to-all-done.1 = f32[6,3,8,192]{3,2,1,0:T(8,128)S(1)} async-done(((f32[6,3,8,192]{3,2,1,0:T(8,128)}), f32[6,3,8,192]{3,2,1,0:T(8,128)S(1)}, u32[]{:S(2)}, u32[]{:S(2)}) %all-to-all-start.1) | async-done | bytes 110624 | tf_op jit(solution)/shard_map/all_to_all | solution.py:215
  98.4 6.1 %collective-permute-done.4 = f32[3,2,4,8,192]{4,3,1,0,2:T(8,128)S(1)} collective-permute-done((f32[3,2,4,8,192]{4,3,1,0,2:T(8,128)S(1)}, f32[3,2,4,8,192]{4,3,1,0,2:T(8,128)S(1)}, u32[]{:S(2)}, u32[]{:S(2)}) %collective-permute-start.4) | collective-permute-done | bytes 147488 | tf_op jit(solution)/shard_map/ppermute | solution.py:240
  104.5 3.0 collective-permute-start.5
  107.5 32.3 %all-reduce.12.cloned.1.call-done = f32[3,2,4,8,192]{4,3,0,2,1:T(8,128)} async-done(((f32[3,2,4,8,192]{4,3,0,2,1:T(8,128)}), f32[3,2,4,8,192]{4,3,0,2,1:T(8,128)}) %all-reduce.12.cloned.1.call-update) | async-done | bytes 147472
  139.8 1.5 constant_dynamic-slice_fusion.5
  141.3 10.7 %all-reduce.7 = (f32[3,2,1,8,192]{4,3,0,2,1:T(8,128)S(1)}, f32[3,2,1,8,1]{3,1,4,0,2:T(2,128)S(1)}, f32[3,2,4,8,1]{3,1,4,0,2:T(2,128)S(1)}) all-reduce(f32[3,2,1,8,192]{4,3,0,2,1:T(8,128)S(1)} %constant_dynamic-slice_fusion.5, f32[3,2,1,8,1]{3,1,4,0,2:T(2,128)S(1)} %constant_dynamic-slice_fusion.4, ...), channel_id=1, replica_groups=mesh['face'=2,'fy'=4,'fx'=4] {'fy'}, use_global_device_ids=true, to_apply=%region_0.1 | all-reduce | flops 9456 | bytes 75648 | tf_op jit(solution)/shard_map/psum | solution.py:237
  154.1 19.5 %reduce-scatter.7.cloned.1.call-done = f32[3,2,1,8,192]{4,3,1,0,2:T(8,128)} async-done(((f32[3,2,4,8,192]{4,3,1,0,2:T(8,128)}), f32[3,2,1,8,192]{4,3,1,0,2:T(8,128)}) %reduce-scatter.7.cloned.1.call-update) | async-done | bytes 36880 | tf_op jit(solution)/shard_map/reduce_scatter | solution.py:244
  179.0 4.5 %collective-permute-start.12 = (f32[3,8,1,192]{3,2,0,1:T(1,128)S(1)}, f32[3,8,1,192]{3,2,0,1:T(1,128)S(1)}, u32[]{:S(2)}, u32[]{:S(2)}) collective-permute-start(f32[3,8,1,192]{3,2,0,1:T(1,128)S(1)} %get-tuple-element.230), channel_id=1, source_target_pairs={{0,1},{1,2},{2,3},{4,5},{5,6},{6,7},{8,9},{9,10},{10,11},{12,13},{... | collective-permute-start | bytes 55304 | tf_op jit(solution)/shard_map/ppermute | solution.py:19
  183.6 1.5 collective-permute-done.12
  186.5 3.2 collective-permute-start.14
  191.3 3.4 all-to-all-start.4
  195.5 4.0 all-to-all-done.4
  199.4 3.4 all-to-all-start.5
  203.4 4.1 %all-to-all-done.5 = f32[6,3,8,192]{3,2,1,0:T(8,128)S(1)} async-done(((f32[6,3,8,192]{3,2,1,0:T(8,128)}), f32[6,3,8,192]{3,2,1,0:T(8,128)S(1)}, u32[]{:S(2)}, u32[]{:S(2)}) %all-to-all-start.5) | async-done | bytes 110624 | tf_op jit(solution)/shard_map/all_to_all | solution.py:215
  209.0 2.4 collective-permute-start.16
  212.4 2.6 collective-permute-done.16
  215.1 3.1 collective-permute-start.17
  218.2 31.4 %all-reduce.14.cloned.1.call-done = f32[3,2,4,8,192]{4,3,0,2,1:T(8,128)} async-done(((f32[3,2,4,8,192]{4,3,0,2,1:T(8,128)}), f32[3,2,4,8,192]{4,3,0,2,1:T(8,128)}) %all-reduce.14.cloned.1.call-update) | async-done | bytes 147472
  249.6 1.5 constant_dynamic-slice_fusion.3
  251.1 10.5 %psum.34 = f32[3,2,1,8,192]{4,3,0,2,1:T(8,128)S(1)} all-reduce(f32[3,2,1,8,192]{4,3,0,2,1:T(8,128)S(1)} %constant_dynamic-slice_fusion.3), channel_id=1, replica_groups=mesh['face'=2,'fy'=4,'fx'=4] {'fy'}, use_global_device_ids=true, to_apply=%region_6.7 | all-reduce | flops 9216 | bytes 73728 | tf_op jit(solution)/shard_map/psum | solution.py:237
  262.4 19.7 %reduce-scatter.9.cloned.1.call-done = f32[3,2,1,8,192]{4,3,1,0,2:T(8,128)} async-done(((f32[3,2,4,8,192]{4,3,1,0,2:T(8,128)}), f32[3,2,1,8,192]{4,3,1,0,2:T(8,128)}) %reduce-scatter.9.cloned.1.call-update) | async-done | bytes 36880 | tf_op jit(solution)/shard_map/reduce_scatter | solution.py:244
  287.5 4.5 %collective-permute-start.18 = (f32[3,8,1,192]{3,2,0,1:T(1,128)S(1)}, f32[3,8,1,192]{3,2,0,1:T(1,128)S(1)}, u32[]{:S(2)}, u32[]{:S(2)}) collective-permute-start(f32[3,8,1,192]{3,2,0,1:T(1,128)S(1)} %get-tuple-element.226), channel_id=1, source_target_pairs={{0,1},{1,2},{2,3},{4,5},{5,6},{6,7},{8,9},{9,10},{10,11},{12,13},{... | collective-permute-start | bytes 55304 | tf_op jit(solution)/shard_map/ppermute | solution.py:19
  292.1 1.5 collective-permute-done.18
  295.0 3.0 collective-permute-start.20
  299.7 3.4 all-to-all-start.6
  303.9 4.0 all-to-all-done.6
  307.9 3.4 all-to-all-start.7
  311.8 4.1 %all-to-all-done.7 = f32[6,3,8,192]{3,2,1,0:T(8,128)S(1)} async-done(((f32[6,3,8,192]{3,2,1,0:T(8,128)}), f32[6,3,8,192]{3,2,1,0:T(8,128)S(1)}, u32[]{:S(2)}, u32[]{:S(2)}) %all-to-all-start.7) | async-done | bytes 110624 | tf_op jit(solution)/shard_map/all_to_all | solution.py:215
  317.5 2.4 collective-permute-start.22
  320.9 2.6 collective-permute-done.22
  323.5 3.1 collective-permute-start.23
  326.7 31.4 %all-reduce.16.cloned.1.call-done = f32[3,2,4,8,192]{4,3,0,2,1:T(8,128)} async-done(((f32[3,2,4,8,192]{4,3,0,2,1:T(8,128)}), f32[3,2,4,8,192]{4,3,0,2,1:T(8,128)}) %all-reduce.16.cloned.1.call-update) | async-done | bytes 147472
  358.1 1.5 constant_dynamic-slice_fusion.2
  359.6 10.5 %psum.35 = f32[3,2,1,8,192]{4,3,0,2,1:T(8,128)S(1)} all-reduce(f32[3,2,1,8,192]{4,3,0,2,1:T(8,128)S(1)} %constant_dynamic-slice_fusion.2), channel_id=1, replica_groups=mesh['face'=2,'fy'=4,'fx'=4] {'fy'}, use_global_device_ids=true, to_apply=%region_9.10 | all-reduce | flops 9216 | bytes 73728 | tf_op jit(solution)/shard_map/psum | solution.py:237
  370.9 19.7 %reduce-scatter.11.cloned.1.call-done = f32[3,2,1,8,192]{4,3,1,0,2:T(8,128)} async-done(((f32[3,2,4,8,192]{4,3,1,0,2:T(8,128)}), f32[3,2,1,8,192]{4,3,1,0,2:T(8,128)}) %reduce-scatter.11.cloned.1.call-update) | async-done | bytes 36880 | tf_op jit(solution)/shard_map/reduce_scatter | solution.py:244
  (289 shorter events, 55.4 us)
Async XLA Ops:
  7.4 19.6 %copy-start = (s32[6,4]{0,1:T(4,128)S(1)}, s32[6,4]{0,1:T(4,128)}, u32[]{:S(2)}) copy-start(s32[6,4]{0,1:T(4,128)} %param.55) | copy-start | bytes 292
  7.4 1.8 copy-start.1
  8.1 1.0 copy-start.3
  9.5 0.7 copy-start.4
  11.2 0.7 copy-start.9
  11.2 0.7 copy-start.2
  12.0 0.7 copy-start.5
  13.0 60.1 %collective-permute-start.1 = (f32[3,8,1,192]{3,2,1,0:T(1,128)S(1)}, f32[3,8,1,192]{3,2,1,0:T(1,128)S(1)}, u32[]{:S(2)}, u32[]{:S(2)}) collective-permute-start(f32[3,8,1,192]{3,2,1,0:T(1,128)S(1)} %slice.903), channel_id=1, source_target_pairs={{1,0},{2,1},{3,2},{5,4},{6,5},{7,6},{9,8},{10,9},{11,10},{13,12},{... | collective-permute-start | bytes 55304 | tf_op jit(solution)/shard_map/ppermute | solution.py:21
  14.4 58.8 %collective-permute-start = (f32[3,8,1,192]{3,2,0,1:T(1,128)S(1)}, f32[3,8,1,192]{3,2,0,1:T(1,128)S(1)}, u32[]{:S(2)}, u32[]{:S(2)}) collective-permute-start(f32[3,8,1,192]{3,2,0,1:T(1,128)S(1)} %slice.902), channel_id=1, source_target_pairs={{0,1},{1,2},{2,3},{4,5},{5,6},{6,7},{8,9},{9,10},{10,11},{12,13},{... | collective-permute-start | bytes 55304 | tf_op jit(solution)/shard_map/ppermute | solution.py:19
  20.1 10.9 %collective-permute-start.7 = (f32[3,8,1,1]{2,1,0,3:T(8,128)S(1)}, f32[3,8,1,1]{2,1,0,3:T(8,128)S(1)}, u32[]{:S(2)}, u32[]{:S(2)}) collective-permute-start(f32[3,8,1,1]{2,1,0,3:T(8,128)S(1)} %get-tuple-element.269), channel_id=1, source_target_pairs={{1,0},{2,1},{3,2},{5,4},{6,5},{7,6},{9,8},{10,9},{11,10},{13,12},{... | collective-permute-start | bytes 296 | tf_op jit(solution)/shard_map/ppermute | solution.py:21
  21.4 9.6 %collective-permute-start.6 = (f32[3,8,1,1]{2,1,0,3:T(8,128)S(1)}, f32[3,8,1,1]{2,1,0,3:T(8,128)S(1)}, u32[]{:S(2)}, u32[]{:S(2)}) collective-permute-start(f32[3,8,1,1]{2,1,0,3:T(8,128)S(1)} %get-tuple-element.268), channel_id=1, source_target_pairs={{0,1},{1,2},{2,3},{4,5},{5,6},{6,7},{8,9},{9,10},{10,11},{12,13},{... | collective-permute-start | bytes 296 | tf_op jit(solution)/shard_map/ppermute | solution.py:19
  26.0 0.7 copy-start.6
  28.3 0.7 copy-start.8
  28.9 0.7 copy-start.7
  31.1 4.3 %collective-permute-start.9 = (f32[3,1,8,1]{2,1,0,3:T(1,128)S(1)}, f32[3,1,8,1]{2,1,0,3:T(1,128)S(1)}, u32[]{:S(2)}, u32[]{:S(2)}) collective-permute-start(f32[3,1,8,1]{2,1,0,3:T(1,128)S(1)} %get-tuple-element.267), channel_id=1, source_target_pairs={{4,0},{8,4},{12,8},{5,1},{9,5},{13,9},{6,2},{10,6},{14,10},{7,3},{... | collective-permute-start | bytes 296 | tf_op jit(solution)/shard_map/ppermute | solution.py:21
  32.4 3.8 collective-permute-start.8
  37.2 7.0 %all-to-all-start.2 = ((f32[6,3,8,1]{2,3,1,0:T(1,128)}), f32[6,3,8,1]{2,3,1,0:T(1,128)S(1)}, u32[]{:S(2)}, u32[]{:S(2)}) async-start(f32[6,3,8,1]{2,3,1,0:T(1,128)} %broadcast_multiply_fusion.7), calls=%async_computation.3 | async-start | bytes 18432 | tf_op jit(solution)/shard_map/all_to_all | solution.py:214
  44.2 7.0 %all-to-all-start.3 = ((f32[6,3,8,1]{2,3,1,0:T(1,128)}), f32[6,3,8,1]{2,3,1,0:T(1,128)S(1)}, u32[]{:S(2)}, u32[]{:S(2)}) async-start(f32[6,3,8,1]{2,3,1,0:T(1,128)} %broadcast_multiply_fusion.6), calls=%async_computation.4 | async-start | bytes 18432 | tf_op jit(solution)/shard_map/all_to_all | solution.py:215
  52.8 20.3 %collective-permute-start.10 = (f32[3,2,4,8,1]{3,1,4,0,2:T(2,128)S(1)}, f32[3,2,4,8,1]{3,1,4,0,2:T(2,128)S(1)}, u32[]{:S(2)}, u32[]{:S(2)}) collective-permute-start(f32[3,2,4,8,1]{3,1,4,0,2:T(2,128)S(1)} %copy.291), channel_id=1, source_target_pairs={{0,1},{1,0},{2,3},{3,2},{4,5},{5,4},{6,7},{7,6},{8,9},{9,8},{10,11... | collective-permute-start | bytes 2312 | tf_op jit(solution)/shard_map/ppermute | solution.py:240
  73.1 5.3 %collective-permute-start.11 = (f32[3,2,4,8,1]{3,1,4,0,2:T(2,128)S(1)}, f32[3,2,4,8,1]{3,1,4,0,2:T(2,128)S(1)}, u32[]{:S(2)}, u32[]{:S(2)}) collective-permute-start(f32[3,2,4,8,1]{3,1,4,0,2:T(2,128)S(1)} %copy_add_fusion), channel_id=1, source_target_pairs={{0,2},{1,3},{2,0},{3,1},{4,6},{5,7},{6,4},{7,5},{8,10},{9,11},{10,... | collective-permute-start | bytes 2312 | tf_op jit(solution)/shard_map/ppermute | solution.py:240
  73.3 5.1 %collective-permute-start.3 = (f32[3,1,8,192]{3,2,1,0:T(8,128)S(1)}, f32[3,1,8,192]{3,2,1,0:T(8,128)S(1)}, u32[]{:S(2)}, u32[]{:S(2)}) collective-permute-start(f32[3,1,8,192]{3,2,1,0:T(8,128)S(1)} %slice.905), channel_id=1, source_target_pairs={{4,0},{8,4},{12,8},{5,1},{9,5},{13,9},{6,2},{10,6},{14,10},{7,3},{... | collective-permute-start | bytes 55304 | tf_op jit(solution)/shard_map/ppermute | solution.py:21
  74.7 3.9 collective-permute-start.2
  79.4 8.0 %all-to-all-start = ((f32[6,3,8,192]{3,2,1,0:T(8,128)}), f32[6,3,8,192]{3,2,1,0:T(8,128)S(1)}, u32[]{:S(2)}, u32[]{:S(2)}) async-start(f32[6,3,8,192]{3,2,1,0:T(8,128)} %broadcast_multiply_fusion.5), calls=%async_computation | async-start | bytes 294912 | tf_op jit(solution)/shard_map/all_to_all | solution.py:214
  87.4 8.0 %all-to-all-start.1 = ((f32[6,3,8,192]{3,2,1,0:T(8,128)}), f32[6,3,8,192]{3,2,1,0:T(8,128)S(1)}, u32[]{:S(2)}, u32[]{:S(2)}) async-start(f32[6,3,8,192]{3,2,1,0:T(8,128)} %broadcast_multiply_fusion.4), calls=%async_computation.1 | async-start | bytes 294912 | tf_op jit(solution)/shard_map/all_to_all | solution.py:215
  90.8 49.0 %all-reduce.12.cloned.1.call-start = ((), (), s32[]{:S(2)}) async-start(), calls=%async_computation.14 | async-start | bytes 393216
  97.0 7.5 %collective-permute-start.4 = (f32[3,2,4,8,192]{4,3,1,0,2:T(8,128)S(1)}, f32[3,2,4,8,192]{4,3,1,0,2:T(8,128)S(1)}, u32[]{:S(2)}, u32[]{:S(2)}) collective-permute-start(f32[3,2,4,8,192]{4,3,1,0,2:T(8,128)S(1)} %copy.281), channel_id=1, source_target_pairs={{0,1},{1,0},{2,3},{3,2},{4,5},{5,4},{6,7},{7,6},{8,9},{9,8},{10,11... | collective-permute-start | bytes 442376 | tf_op jit(solution)/shard_map/ppermute | solution.py:240
  98.3 75.4 %reduce-scatter.7.cloned.1.call-start = ((), (), s32[]{:S(2)}) async-start(), calls=%async_computation.11 | async-start | bytes 245760 | tf_op jit(solution)/shard_map/reduce_scatter | solution.py:244
  104.5 48.6 %collective-permute-start.5 = (f32[3,2,4,8,192]{4,3,1,0,2:T(8,128)S(1)}, f32[3,2,4,8,192]{4,3,1,0,2:T(8,128)S(1)}, u32[]{:S(2)}, u32[]{:S(2)}) collective-permute-start(f32[3,2,4,8,192]{4,3,1,0,2:T(8,128)S(1)} %copy_add_fusion.3), channel_id=1, source_target_pairs={{0,2},{1,3},{2,0},{3,1},{4,6},{5,7},{6,4},{7,5},{8,10},{9,11},{10,... | collective-permute-start | bytes 442376 | tf_op jit(solution)/shard_map/ppermute | solution.py:240
  177.7 5.9 %collective-permute-start.13 = (f32[3,8,1,192]{3,2,0,1:T(1,128)S(1)}, f32[3,8,1,192]{3,2,0,1:T(1,128)S(1)}, u32[]{:S(2)}, u32[]{:S(2)}) collective-permute-start(f32[3,8,1,192]{3,2,0,1:T(1,128)S(1)} %get-tuple-element.231), channel_id=1, source_target_pairs={{1,0},{2,1},{3,2},{5,4},{6,5},{7,6},{9,8},{10,9},{11,10},{13,12},{... | collective-permute-start | bytes 55304 | tf_op jit(solution)/shard_map/ppermute | solution.py:21
  179.0 6.1 %collective-permute-start.12 = (f32[3,8,1,192]{3,2,0,1:T(1,128)S(1)}, f32[3,8,1,192]{3,2,0,1:T(1,128)S(1)}, u32[]{:S(2)}, u32[]{:S(2)}) collective-permute-start(f32[3,8,1,192]{3,2,0,1:T(1,128)S(1)} %get-tuple-element.230), channel_id=1, source_target_pairs={{0,1},{1,2},{2,3},{4,5},{5,6},{6,7},{8,9},{9,10},{10,11},{12,13},{... | collective-permute-start | bytes 55304 | tf_op jit(solution)/shard_map/ppermute | solution.py:19
  185.2 4.5 %collective-permute-start.15 = (f32[3,1,8,192]{3,2,0,1:T(8,128)S(1)}, f32[3,1,8,192]{3,2,0,1:T(8,128)S(1)}, u32[]{:S(2)}, u32[]{:S(2)}) collective-permute-start(f32[3,1,8,192]{3,2,0,1:T(8,128)S(1)} %get-tuple-element.229), channel_id=1, source_target_pairs={{4,0},{8,4},{12,8},{5,1},{9,5},{13,9},{6,2},{10,6},{14,10},{7,3},{... | collective-permute-start | bytes 55304 | tf_op jit(solution)/shard_map/ppermute | solution.py:21
  186.5 3.9 collective-permute-start.14
  191.3 8.1 %all-to-all-start.4 = ((f32[6,3,8,192]{3,2,1,0:T(8,128)}), f32[6,3,8,192]{3,2,1,0:T(8,128)S(1)}, u32[]{:S(2)}, u32[]{:S(2)}) async-start(f32[6,3,8,192]{3,2,1,0:T(8,128)} %broadcast_multiply_fusion.3), calls=%async_computation.5 | async-start | bytes 294912 | tf_op jit(solution)/shard_map/all_to_all | solution.py:214
  199.4 8.0 %all-to-all-start.5 = ((f32[6,3,8,192]{3,2,1,0:T(8,128)}), f32[6,3,8,192]{3,2,1,0:T(8,128)S(1)}, u32[]{:S(2)}, u32[]{:S(2)}) async-start(f32[6,3,8,192]{3,2,1,0:T(8,128)} %broadcast_multiply_fusion.2), calls=%async_computation.6 | async-start | bytes 294912 | tf_op jit(solution)/shard_map/all_to_all | solution.py:215
  202.9 46.7 %all-reduce.14.cloned.1.call-start = ((), (), s32[]{:S(2)}) async-start(), calls=%async_computation.15 | async-start | bytes 393216
  209.0 6.0 %collective-permute-start.16 = (f32[3,2,4,8,192]{4,3,1,0,2:T(8,128)S(1)}, f32[3,2,4,8,192]{4,3,1,0,2:T(8,128)S(1)}, u32[]{:S(2)}, u32[]{:S(2)}) collective-permute-start(f32[3,2,4,8,192]{4,3,1,0,2:T(8,128)S(1)} %copy.321), channel_id=1, source_target_pairs={{0,1},{1,0},{2,3},{3,2},{4,5},{5,4},{6,7},{7,6},{8,9},{9,8},{10,11... | collective-permute-start | bytes 442376 | tf_op jit(solution)/shard_map/ppermute | solution.py:240
  212.4 69.8 %reduce-scatter.9.cloned.1.call-start = ((), (), s32[]{:S(2)}) async-start(), calls=%async_computation.12 | async-start | bytes 245760 | tf_op jit(solution)/shard_map/reduce_scatter | solution.py:244
  215.1 46.5 %collective-permute-start.17 = (f32[3,2,4,8,192]{4,3,1,0,2:T(8,128)S(1)}, f32[3,2,4,8,192]{4,3,1,0,2:T(8,128)S(1)}, u32[]{:S(2)}, u32[]{:S(2)}) collective-permute-start(f32[3,2,4,8,192]{4,3,1,0,2:T(8,128)S(1)} %copy_add_fusion.2), channel_id=1, source_target_pairs={{0,2},{1,3},{2,0},{3,1},{4,6},{5,7},{6,4},{7,5},{8,10},{9,11},{10,... | collective-permute-start | bytes 442376 | tf_op jit(solution)/shard_map/ppermute | solution.py:240
  286.2 5.9 %collective-permute-start.19 = (f32[3,8,1,192]{3,2,0,1:T(1,128)S(1)}, f32[3,8,1,192]{3,2,0,1:T(1,128)S(1)}, u32[]{:S(2)}, u32[]{:S(2)}) collective-permute-start(f32[3,8,1,192]{3,2,0,1:T(1,128)S(1)} %get-tuple-element.227), channel_id=1, source_target_pairs={{1,0},{2,1},{3,2},{5,4},{6,5},{7,6},{9,8},{10,9},{11,10},{13,12},{... | collective-permute-start | bytes 55304 | tf_op jit(solution)/shard_map/ppermute | solution.py:21
  287.5 6.1 %collective-permute-start.18 = (f32[3,8,1,192]{3,2,0,1:T(1,128)S(1)}, f32[3,8,1,192]{3,2,0,1:T(1,128)S(1)}, u32[]{:S(2)}, u32[]{:S(2)}) collective-permute-start(f32[3,8,1,192]{3,2,0,1:T(1,128)S(1)} %get-tuple-element.226), channel_id=1, source_target_pairs={{0,1},{1,2},{2,3},{4,5},{5,6},{6,7},{8,9},{9,10},{10,11},{12,13},{... | collective-permute-start | bytes 55304 | tf_op jit(solution)/shard_map/ppermute | solution.py:19
  293.7 4.3 %collective-permute-start.21 = (f32[3,1,8,192]{3,2,0,1:T(8,128)S(1)}, f32[3,1,8,192]{3,2,0,1:T(8,128)S(1)}, u32[]{:S(2)}, u32[]{:S(2)}) collective-permute-start(f32[3,1,8,192]{3,2,0,1:T(8,128)S(1)} %get-tuple-element.225), channel_id=1, source_target_pairs={{4,0},{8,4},{12,8},{5,1},{9,5},{13,9},{6,2},{10,6},{14,10},{7,3},{... | collective-permute-start | bytes 55304 | tf_op jit(solution)/shard_map/ppermute | solution.py:21
  295.0 3.9 collective-permute-start.20
  299.7 8.1 %all-to-all-start.6 = ((f32[6,3,8,192]{3,2,1,0:T(8,128)}), f32[6,3,8,192]{3,2,1,0:T(8,128)S(1)}, u32[]{:S(2)}, u32[]{:S(2)}) async-start(f32[6,3,8,192]{3,2,1,0:T(8,128)} %broadcast_multiply_fusion.1), calls=%async_computation.8 | async-start | bytes 294912 | tf_op jit(solution)/shard_map/all_to_all | solution.py:214
  307.9 8.0 %all-to-all-start.7 = ((f32[6,3,8,192]{3,2,1,0:T(8,128)}), f32[6,3,8,192]{3,2,1,0:T(8,128)S(1)}, u32[]{:S(2)}, u32[]{:S(2)}) async-start(f32[6,3,8,192]{3,2,1,0:T(8,128)} %broadcast_multiply_fusion), calls=%async_computation.9 | async-start | bytes 294912 | tf_op jit(solution)/shard_map/all_to_all | solution.py:215
  311.3 46.7 %all-reduce.16.cloned.1.call-start = ((), (), s32[]{:S(2)}) async-start(), calls=%async_computation.16 | async-start | bytes 393216
  317.5 6.0 %collective-permute-start.22 = (f32[3,2,4,8,192]{4,3,1,0,2:T(8,128)S(1)}, f32[3,2,4,8,192]{4,3,1,0,2:T(8,128)S(1)}, u32[]{:S(2)}, u32[]{:S(2)}) collective-permute-start(f32[3,2,4,8,192]{4,3,1,0,2:T(8,128)S(1)} %copy.339), channel_id=1, source_target_pairs={{0,1},{1,0},{2,3},{3,2},{4,5},{5,4},{6,7},{7,6},{8,9},{9,8},{10,11... | collective-permute-start | bytes 442376 | tf_op jit(solution)/shard_map/ppermute | solution.py:240
  320.8 69.8 %reduce-scatter.11.cloned.1.call-start = ((), (), s32[]{:S(2)}) async-start(), calls=%async_computation.13 | async-start | bytes 245760 | tf_op jit(solution)/shard_map/reduce_scatter | solution.py:244
  323.5 46.5 %collective-permute-start.23 = (f32[3,2,4,8,192]{4,3,1,0,2:T(8,128)S(1)}, f32[3,2,4,8,192]{4,3,1,0,2:T(8,128)S(1)}, u32[]{:S(2)}, u32[]{:S(2)}) collective-permute-start(f32[3,2,4,8,192]{4,3,1,0,2:T(8,128)S(1)} %copy_add_fusion.1), channel_id=1, source_target_pairs={{0,2},{1,3},{2,0},{3,1},{4,6},{5,7},{6,4},{7,5},{8,10},{9,11},{10,... | collective-permute-start | bytes 442376 | tf_op jit(solution)/shard_map/ppermute | solution.py:240
Sparse Core Ops, SparseCore 0:
  98.4 41.3 all-reduce.11
  212.5 37.0 all-reduce.13
  320.9 37.0 all-reduce.15
Sparse Core Ops, SparseCore 1:
  153.9 19.7 reduce-scatter.6
  262.4 19.7 reduce-scatter.8
  370.9 19.7 reduce-scatter.10
